TPU v7x, 32 devices: a whole 2x2x4 slice. The times are simulated.
32 devices in a mesh: samp: 4 (over x, core), var: 8 (over z, y).
Axes of the slice: x: 2, y: 2, z: 4, core: 2. Of those that a mesh axis runs over, the one named last changes fastest.
Arguments:
- phenotype: bfloat16 [8192, 256], P(('samp', 'var')), may hold values from -1500 to 1500
- inverse_blocks: float32 [32, 256, 256], P(('samp', 'var')), may hold values from -1 to 2, as said below
- bin_sizes: int32 [4, 8], P('samp', 'var'), may hold values from 128 to 256, as said below
- slot_of: int32 [6144], P('samp'), may hold values from 0 to 2047, as said below
- dosages: bfloat16 [6144, 8192], P('samp', 'var'), may hold values from 0 to 2
Outputs:
- z_scores: float32 [8192, 256], P('var', 'samp')
Inputs may be any that keep to these rules, and one draw needn't show every extreme that they name: `bin_sizes`: within each row (one sample shard) the sizes sum to 192 times the row's length, and at least one bin is full. `slot_of`: within each sample shard the samples occupy exactly the live slots: slot v * 256 + r with r < bin_sizes of bin v, each once. `inverse_blocks`: each block is symmetric positive definite.
All inputs are finite; a program needn't handle non-finite values.
Results may differ from a plain program's by a relative error of at most 0.0041.
Values may be sent and summed in bfloat16 or wider, within the bound.
No kernel may reach another device: no remote copies, remote signals or barrier semaphores. Data moves between devices by JAX's collectives and lax.ppermute only.
A program may use at most 128 MiB of HBM per device.

v0:
```python
import jax
import jax.numpy as jnp
from jax import lax
from jax.sharding import PartitionSpec as P

epsilon = 1e-06


def local(phenotype, inverse_blocks, bin_sizes, slot_of, dosages):
    bin_width = inverse_blocks.shape[1]
    position = jnp.arange(bin_width, dtype=jnp.int32)
    live_mask = (position < bin_sizes.reshape(())).astype(jnp.float32)[:, None]
    masked_pheno = phenotype.astype(jnp.float32) * live_mask
    whitened = (
        jnp.dot(
            inverse_blocks[0],
            masked_pheno,
            precision=lax.Precision.HIGHEST,
            preferred_element_type=jnp.float32,
        )
        * live_mask
    )
    trait_scale = lax.psum(jnp.sum(masked_pheno * whitened, axis=0), ("samp", "var"))
    white_rows = whitened.astype(jnp.bfloat16)
    slot_weight = jnp.diagonal(inverse_blocks[0]).astype(jnp.bfloat16)
    gathered, weights_all = (
        lax.all_gather(white_rows, "var", axis=0, tiled=True),
        lax.all_gather(slot_weight, "var", axis=0, tiled=True),
    )
    picked = jnp.take(gathered, slot_of, axis=0)
    score_part = lax.dot_general(
        dosages, picked, (((0,), (0,)), ((), ())), preferred_element_type=jnp.float32
    )
    sample_weight = jnp.take(weights_all, slot_of).astype(jnp.float32)
    variance = jnp.dot(
        sample_weight, dosages.astype(jnp.float32) ** 2, precision=lax.Precision.HIGHEST
    )
    trait_count = phenotype.shape[1] // lax.axis_size("samp")
    trait_start = lax.axis_index("samp") * trait_count
    score_share = lax.psum_scatter(score_part, "samp", scatter_dimension=1, tiled=True)
    variance_all = lax.psum(variance, "samp")
    scale_share = lax.dynamic_slice_in_dim(trait_scale, trait_start, trait_count, 0)
    sample_count = slot_of.shape[0] * lax.axis_size("samp")
    return score_share / jnp.sqrt(
        variance_all[:, None] * scale_share[None, :] / sample_count + epsilon
    )


def solution(mesh):
    in_specs = (
        P(("samp", "var"), None),
        P(("samp", "var"), None, None),
        P("samp", "var"),
        P("samp"),
        P("samp", "var"),
    )
    out_specs = P("var", "samp")
    return jax.shard_map(local, mesh=mesh, in_specs=in_specs, out_specs=out_specs, check_vma=False)
```

profile of v0, /device:TPU:0, one launch (start us, length us, event | category | flops | bytes accessed | tf_op | source)
XLA Modules:
  0.0 117.7 jit_solution(12042622595984199187)
XLA Ops:
  6.5 0.0 copy-start
  6.5 0.0 copy-start.2
  6.5 0.0 all-gather.3.cloned.1.call-start
  7.2 0.3 copy-done
  7.5 2.1 %multiply_reduce_fusion = (f32[256]{0:T(256)S(1)}, bf16[256,256]{1,0:T(8,128)(2,1)}) fusion(bf16[256,256]{1,0:T(8,128)(2,1)} %param.5, f32[256]{0:T(256)S(1)} %compare_convert_fusion, f32[1,256,256]{2,1,0:T(8,128)S(1)} %copy-done), kind=kOutput, calls=%fused_computation.13 | convolution fusion | flops 201850624 | bytes 526336 | tf_op jit(solution)/shard_map/dot_general | solution.py:15
  9.6 0.0 all-gather.3.cloned.1.call-update
  9.6 0.0 reduce-scatter.2.cloned.1.call-start
  9.7 2.3 %gather_fusion.1 = bf16[256]{0:T(256)(128)(2,1)S(1)} fusion(f32[256,256]{1,0:T(8,128)S(1)} %bitcast.17, s32[256]{0:T(256)S(1)} %bitcast.19), kind=kCustom, calls=%fused_computation.1 | custom fusion | bytes 3072 | tf_op jit(solution)/shard_map/jit(diagonal)/cond/branch_0_fun/gather | solution.py:25
  12.1 22.3 %all-gather = bf16[8,1,256]{2,1,0:T(2,128)(2,1)S(1)} all-gather(bf16[1,1,256]{2,1,0:T(2,128)(2,1)S(1)} %reshape.40), channel_id=1, replica_groups=mesh['samp'=4,'var'=8] {'var'}, dimensions={0}, use_global_device_ids=true | all-gather | bytes 4608 | tf_op jit(solution)/shard_map/all_gather | solution.py:28
  34.4 0.7 compare_select_fusion
  35.1 9.5 %gather_fusion.2 = bf16[1536]{0:T(1024)(128)(2,1)S(1)} fusion(bf16[2048]{0:T(1024)(128)(2,1)S(1)} %bitcast.18, s32[2048]{0:T(1024)S(1)} %pad_clamp_fusion), kind=kCustom, calls=%fused_computation.2 | custom fusion | bytes 12288 | tf_op jit(solution)/shard_map/jit(_take)/gather | solution.py:34
  44.6 0.0 copy-done.2
  44.6 0.0 copy-start.1
  44.6 8.2 %all-gather.3.cloned.1.call-done = bf16[2048,256]{1,0:T(8,128)(2,1)} async-done(((bf16[256,256]{1,0:T(8,128)(2,1)}), bf16[2048,256]{1,0:T(8,128)(2,1)}) %all-gather.3.cloned.1.call-update) | async-done | bytes 1048592 | tf_op jit(solution)/shard_map/all_gather | solution.py:27
  52.8 5.9 %gather_fusion = bf16[1536,256]{1,0:T(8,128)(2,1)} fusion(bf16[2048,256]{1,0:T(8,128)(2,1)} %all-gather.3.cloned.1.call-done, s32[2048]{0:T(1024)S(1)} %pad_clamp_fusion), kind=kCustom, calls=%fused_computation | custom fusion | bytes 1579008 | tf_op jit(solution)/shard_map/jit(_take)/gather | solution.py:30
  58.7 0.0 copy-done.1
  58.7 3.2 %convolution_bitcast_fusion = f32[1024,256]{0,1:T(8,128)} fusion(bf16[1536,1024]{1,0:T(8,128)(2,1)S(1)} %copy-done.1, bf16[1536,256]{1,0:T(8,128)(2,1)} %gather_fusion, pred[1536]{0:T(1024)(128)(4,1)S(1)} %get-tuple-element.6), kind=kOutput, calls=%fused_computation.6 | convolution fusion | flops 805699584 | bytes 4982272 | tf_op jit(solution)/shard_map/dot_general | solution.py:31
  61.9 0.0 reduce-scatter.2.cloned.1.call-update
  61.9 38.1 %psum.15 = f32[256]{0:T(256)S(1)} all-reduce(f32[256]{0:T(256)S(1)} %get-tuple-element.7), channel_id=1, replica_groups=mesh['samp'=4,'var'=8] {'samp','var'}, use_global_device_ids=true, to_apply=%region_3.4 | all-reduce | flops 256 | bytes 2048 | tf_op jit(solution)/shard_map/psum | solution.py:23
  100.0 0.1 dynamic_slice.3
  100.1 2.4 %fusion = f32[1,1024]{1,0:T(1,128)S(1)} fusion(bf16[1536,1]{0,1:T(2,128)(2,1)S(1)} %reshape.42, bf16[1536,1024]{1,0:T(8,128)(2,1)S(1)} %copy-done.1), kind=kOutput, calls=%fused_computation.3 | convolution fusion | flops 22020096 | bytes 3152896 | tf_op jit(solution)/shard_map/dot_general | solution.py:35
  102.5 6.5 %psum.14 = f32[1024]{0:T(1024)S(1)} all-reduce(f32[1024]{0:T(1024)S(1)} %bitcast.20), channel_id=1, replica_groups=mesh['samp'=4,'var'=8] {'samp'}, use_global_device_ids=true, to_apply=%region_1.0 | all-reduce | flops 1024 | bytes 8192 | tf_op jit(solution)/shard_map/psum | solution.py:41
  109.0 0.0 reduce-scatter.2.cloned.1.call-done
  109.0 1.8 %rsqrt_multiply_fusion = f32[1024,64]{0,1:T(8,128)} fusion(f32[1024,64]{0,1:T(8,128)} %reduce-scatter.2.cloned.1.call-done, f32[64]{0:T(128)S(1)} %dynamic_slice.3, f32[1024]{0:T(1024)S(1)} %psum.14), kind=kLoop, calls=%fused_computation.12 | loop fusion | flops 262144 | bytes 528640 | tf_op jit(solution)/shard_map/div | solution.py:44
  (8 shorter events, 0.1 us)
Async XLA Ops:
  6.5 1.0 copy-start
  6.5 38.1 %copy-start.2 = (s32[1536]{0:T(1024)S(1)}, s32[1536]{0:T(1024)}, u32[]{:S(2)}) copy-start(s32[1536]{0:T(1024)} %param.8) | copy-start | bytes 18436
  6.5 46.3 %all-gather.3.cloned.1.call-start = ((), (), s32[]{:S(2)}) async-start(), calls=%async_computation.1 | async-start | bytes 1179648 | tf_op jit(solution)/shard_map/all_gather | solution.py:27
  9.6 99.4 %reduce-scatter.2.cloned.1.call-start = ((), (), s32[]{:S(2)}) async-start(), calls=%async_computation.2 | async-start | bytes 1310720 | tf_op jit(solution)/shard_map/reduce_scatter | solution.py:40
  44.6 14.0 %copy-start.1 = (bf16[1536,1024]{1,0:T(8,128)(2,1)S(1)}, bf16[1536,1024]{1,0:T(8,128)(2,1)}, u32[]{:S(2)}) copy-start(bf16[1536,1024]{1,0:T(8,128)(2,1)} %param.9) | copy-start | bytes 9437188
Sparse Core Ops, SparseCore 0:
  9.8 42.9 all-gather.2
  62.0 23.5 reduce-scatter.1
where the time goes:
time: 118 us
  blocking collectives  66.9 us (57%)
  local copies, waits for them, and re-layouts  18 us (15%)
  between operations  14.2 us (12%)
  waiting for transfers between devices  8.19 us (7%)
  matrix products  7.78 us (7%)
  other arithmetic  2.53 us (2%)
    psum x1, blocking collectives, local(): lax.psum(jnp.sum(masked_pheno * whitened, axis=0), ('samp', 'var'))  38.1 us
    all_gather x1, blocking collectives, local(): lax.all_gather(slot_weight, 'var', axis=0, tiled=True)  22.3 us
    gather x1, local copies, waits for them, and re-layouts, local(): sample_weight = jnp.take(weights_all, slot_of).astype(jnp.float32)  9.46 us
    all_gather x1, waiting for transfers between devices, local(): lax.all_gather(white_rows, 'var', axis=0, tiled=True)  8.15 us
    psum x1, blocking collectives, local(): variance_all = lax.psum(variance, 'samp')  6.51 us
    gather x1, local copies, waits for them, and re-layouts, local(): picked = jnp.take(gathered, slot_of, axis=0)  5.86 us
    dot_general x1, matrix products, local(): lax.dot_general(dosages, picked, (((0,), (0,)), ((), ())), preferred_elem...  3.22 us
    dot_general x1, matrix products, local(): jnp.dot(sample_weight, dosages.astype(jnp.float32) ** 2, precision=lax.Pr...  2.45 us
  transfers between devices with their start and end apart: 2, of which 1 were waited for; matrix products, arithmetic and copies ran while one was open for 13% of the time, Pallas kernels for 0%

commit v1 on v0

v1 whole, which is shorter than its diff:
```python
import functools
import math

import jax
import jax.numpy as jnp
from jax import lax
from jax.experimental import pallas as pl
from jax.experimental.pallas import tpu as pltpu
from jax.sharding import PartitionSpec as P

epsilon = 1e-06
F32 = jnp.float32
BF16 = jnp.bfloat16
LANES = 128
EXTRA = 16

VMEM = pl.BlockSpec(memory_space=pltpu.VMEM)
SMEM = pl.BlockSpec(memory_space=pltpu.SMEM)


def split3(value):
    high = value.astype(BF16)
    rest = value - high.astype(F32)
    mid = rest.astype(BF16)
    low = (rest - mid.astype(F32)).astype(BF16)
    return high, mid, low


def join3(high, mid, low):
    return (low.astype(F32) + mid.astype(F32)) + high.astype(F32)


def whiten_kernel(size_ref, pheno_ref, inverse_ref, out_ref):
    width, traits = pheno_ref.shape
    live = lax.broadcasted_iota(jnp.int32, (width, traits), 0) < size_ref[0, 0]
    masked = jnp.where(live, pheno_ref[...].astype(F32), 0.0)
    masked_low = masked.astype(BF16)
    inverse = inverse_ref[0]
    high, mid, low = split3(inverse)
    dot = functools.partial(jnp.dot, preferred_element_type=F32)
    whitened = dot(high, masked_low) + (dot(mid, masked_low) + dot(low, masked_low))
    whitened = jnp.where(live, whitened, 0.0)
    out_ref[:traits, :] = whitened.T.astype(BF16)
    form = jnp.sum(masked * whitened, axis=0, keepdims=True)
    square = lax.broadcasted_iota(jnp.int32, (width, width), 0) == lax.broadcasted_iota(
        jnp.int32, (width, width), 1
    )
    weight = jnp.sum(jnp.where(square, inverse, 0.0), axis=0, keepdims=True)
    high, mid, low = split3(form)
    row = lax.broadcasted_iota(jnp.int32, (EXTRA, width), 0)
    extra = jnp.where(row == 0, weight, 0.0)
    extra = jnp.where(row == 1, high.astype(F32), extra)
    extra = jnp.where(row == 2, mid.astype(F32), extra)
    extra = jnp.where(row == 3, low.astype(F32), extra)
    out_ref[traits:, :] = extra.astype(BF16)


def whiten(bin_sizes, phenotype, inverse_blocks):
    width, traits = phenotype.shape
    return pl.pallas_call(
        whiten_kernel,
        out_shape=jax.ShapeDtypeStruct((traits + EXTRA, width), BF16),
        in_specs=[SMEM, VMEM, VMEM],
        out_specs=VMEM,
        name="whiten",
    )(bin_sizes, phenotype, inverse_blocks)


def arrange_kernel(slot_ref, dosage_ref, out_ref, select_ref):
    rows = out_ref.shape[0]

    @pl.when(pl.program_id(1) == 0)
    def _():
        first = pl.program_id(0) * rows
        step = 256
        for start in range(0, rows, step):
            index = lax.broadcasted_iota(jnp.int32, (step, select_ref.shape[1]), 0)
            hit = index + (first + start) == slot_ref[...]
            select_ref[start : start + step, :] = jnp.where(hit, 1.0, 0.0).astype(BF16)

    out_ref[...] = jnp.dot(
        select_ref[...], dosage_ref[...], preferred_element_type=F32
    ).astype(BF16)


def arrange(slots, dosages, slot_count):
    samples, variants = dosages.shape
    rows = slot_count
    while rows * samples * 2 > 2**24:
        rows //= 2
    columns = 256
    return pl.pallas_call(
        arrange_kernel,
        out_shape=jax.ShapeDtypeStruct((slot_count, variants), BF16),
        grid=(slot_count // rows, variants // columns),
        in_specs=[
            pl.BlockSpec((1, samples), lambda i, j: (0, 0)),
            pl.BlockSpec((samples, columns), lambda i, j: (0, j)),
        ],
        out_specs=pl.BlockSpec((rows, columns), lambda i, j: (i, j)),
        scratch_shapes=[pltpu.VMEM((rows, samples), BF16)],
        cost_estimate=pl.CostEstimate(
            flops=2 * slot_count * samples * variants,
            bytes_accessed=2 * variants * (samples + slot_count),
            transcendentals=0,
        ),
        name="arrange",
    )(slots, dosages)


def accumulate(blocks, dosage_ref, first, score_ref, extra_ref, start):
    traits = score_ref.shape[0]
    width = blocks[0].shape[1]
    variants = dosage_ref.shape[1]
    dot = functools.partial(jnp.dot, preferred_element_type=F32)
    step = 256
    for column in range(0, variants, step):
        columns = slice(column, column + step)
        score = None if start else score_ref[:, columns]
        variance = None if start else extra_ref[:EXTRA, columns]
        for i, block in enumerate(blocks):
            rows = slice((first + i) * width, (first + i + 1) * width)
            dosage = dosage_ref[rows, columns]
            part = dot(block[:traits, :], dosage)
            score = part if score is None else score + part
            wide = dosage.astype(F32)
            square = wide * wide
            high = square.astype(BF16)
            low = (square - high.astype(F32)).astype(BF16)
            weight = block[traits:, :]
            part = dot(weight, high) + dot(weight, low)
            variance = part if variance is None else variance + part
        score_ref[:, columns] = score
        extra_ref[:EXTRA, columns] = variance
    form = None if start else extra_ref[EXTRA : EXTRA + 1, :width]
    for block in blocks:
        tail = block[traits:, :].astype(F32)
        part = (tail[3:4, :] + tail[2:3, :]) + tail[1:2, :]
        form = part if form is None else form + part
    extra_ref[EXTRA : EXTRA + 1, :width] = form


def score_first_kernel(count, *refs):
    blocks, dosage_ref, score_ref, extra_ref = refs[:count], *refs[count:]
    accumulate(blocks, dosage_ref, 0, score_ref, extra_ref, True)


def score_first(blocks, arranged, traits):
    variants = arranged.shape[1]
    count = len(blocks)
    width = blocks[0].shape[1]
    return pl.pallas_call(
        functools.partial(score_first_kernel, count),
        out_shape=(
            jax.ShapeDtypeStruct((traits, variants), F32),
            jax.ShapeDtypeStruct((EXTRA + 8, variants), F32),
        ),
        in_specs=[VMEM] * (count + 1),
        out_specs=(VMEM, VMEM),
        cost_estimate=pl.CostEstimate(
            flops=4 * count * width * traits * variants,
            bytes_accessed=4 * count * width * variants,
            transcendentals=0,
        ),
        name="score_first",
    )(*blocks, arranged)


def put_rows(ref, where, base, value):
    height = value.shape[0]
    for i in range(value.shape[1] // LANES):
        ref[where, base + i * height : base + (i + 1) * height, :] = value[
            :, i * LANES : (i + 1) * LANES
        ]


def pack_extra(extra, traits):
    variants = extra.shape[1]
    rows = [extra[0:1, i * LANES : (i + 1) * LANES] for i in range(variants // LANES)]
    rows += [
        extra[EXTRA : EXTRA + 1, i * LANES : (i + 1) * LANES]
        for i in range(traits // LANES)
    ]
    pad = -len(rows) % EXTRA
    if pad:
        rows.append(jnp.zeros((pad, LANES), F32))
    return jnp.concatenate(rows, axis=0)


def extra_rows(traits, variants):
    return -(-(traits // LANES + variants // LANES) // EXTRA) * EXTRA


def put_extra(ref, where, base, packed):
    rows = packed.shape[0]
    for i, part in enumerate(split3(packed)):
        ref[where, base + i * rows : base + (i + 1) * rows, :] = part


def get_extra(value, base, rows):
    parts = [value[base + i * rows : base + (i + 1) * rows, :] for i in range(3)]
    return join3(*parts)


def score_last_kernel(count, first, chips, cores, *refs):
    core_ref = refs[0]
    blocks = refs[1 : count + 1]
    (
        dosage_ref,
        score_in,
        extra_in,
        send_ref,
        keep_ref,
        extra_keep,
        score_ref,
        extra_ref,
    ) = refs[count + 1 :]
    score_ref[...] = score_in[...]
    extra_ref[...] = extra_in[...]
    accumulate(blocks, dosage_ref, first, score_ref, extra_ref, False)
    traits, variants = score_ref.shape
    share = traits // (chips * cores)
    core = core_ref[0]
    packed = pack_extra(extra_ref[...], traits)
    extra_keep[...] = packed
    body = share * variants // LANES
    for chip in range(chips):
        own = pl.multiple_of((chip * cores + core) * share, share)
        keep_ref[chip * share : (chip + 1) * share, :] = score_ref[pl.ds(own, share), :]
    for hop in range(1, cores):
        other = lax.rem(core + hop, cores)
        for chip in range(chips):
            start = pl.multiple_of((chip * cores + other) * share, share)
            put_rows(
                send_ref,
                hop - 1,
                chip * body,
                score_ref[pl.ds(start, share), :].astype(BF16),
            )
        put_extra(send_ref, hop - 1, chips * body, packed)


def score_last(core, blocks, first, arranged, score, extra, chips, cores):
    traits, variants = score.shape
    count = len(blocks)
    share = traits // (chips * cores)
    rows = extra_rows(traits, variants)
    body = share * variants // LANES
    return pl.pallas_call(
        functools.partial(score_last_kernel, count, first, chips, cores),
        out_shape=(
            jax.ShapeDtypeStruct((cores - 1, chips * body + 3 * rows, LANES), BF16),
            jax.ShapeDtypeStruct((chips * share, variants), F32),
            jax.ShapeDtypeStruct((rows, LANES), F32),
        ),
        in_specs=[SMEM] + [VMEM] * (count + 3),
        out_specs=(VMEM, VMEM, VMEM),
        scratch_shapes=[
            pltpu.VMEM((traits, variants), F32),
            pltpu.VMEM(extra.shape, F32),
        ],
        name="score_last",
    )(core, *blocks, arranged, score, extra)


def middle_kernel(hops, chips, share, *refs):
    chip_ref, keep_ref, extra_ref = refs[:3]
    got = refs[3 : 3 + hops]
    send_ref, own_ref, extra_out = refs[3 + hops :]
    variants = keep_ref.shape[1]
    body = share * variants // LANES
    rows = extra_ref.shape[0]
    me = chip_ref[0]
    packed = extra_ref[...]
    for one in got:
        packed = packed + get_extra(one, chips * body, rows)
    extra_out[...] = packed
    for hop in range(chips):
        chip = lax.rem(me + hop, chips)
        here = pl.multiple_of(chip * share, share)
        for i in range(variants // LANES):
            lanes = slice(i * LANES, (i + 1) * LANES)
            there = pl.multiple_of(chip * body + i * share, share)
            total = keep_ref[pl.ds(here, share), lanes]
            for one in got:
                total = total + one[pl.ds(there, share), :].astype(F32)
            if hop == 0:
                own_ref[:, lanes] = total
            else:
                send_ref[hop - 1, i * share : (i + 1) * share, :] = total.astype(BF16)
        if hop:
            put_extra(send_ref, hop - 1, body, packed)


def middle(chip, keep, extra, got, chips, share):
    variants = keep.shape[1]
    body = share * variants // LANES
    rows = extra.shape[0]
    return pl.pallas_call(
        functools.partial(middle_kernel, len(got), chips, share),
        out_shape=(
            jax.ShapeDtypeStruct((max(chips - 1, 1), body + 3 * rows, LANES), BF16),
            jax.ShapeDtypeStruct((share, variants), F32),
            jax.ShapeDtypeStruct((rows, LANES), F32),
        ),
        in_specs=[SMEM] + [VMEM] * (2 + len(got)),
        out_specs=(VMEM, VMEM, VMEM),
        name="middle",
    )(chip, keep, extra, *got)


def final_kernel(hops, traits, samples, *refs):
    samp_ref, own_ref, extra_ref = refs[:3]
    got = refs[3 : 3 + hops]
    out_ref = refs[3 + hops]
    share, variants = own_ref.shape
    body = share * variants // LANES
    rows = extra_ref.shape[0]
    packed = extra_ref[...]
    for one in got:
        packed = packed + get_extra(one, body, rows)
    base = variants // LANES
    trait = samp_ref[0] * share + lax.broadcasted_iota(jnp.int32, (share, LANES), 0)
    lane = lax.broadcasted_iota(jnp.int32, (share, LANES), 1)
    form = jnp.zeros((share, LANES), F32)
    for i in range(traits // LANES):
        form = form + jnp.where(
            lane + i * LANES == trait, packed[base + i : base + i + 1, :], 0.0
        )
    form = jnp.sum(form, axis=1, keepdims=True)
    for i in range(variants // LANES):
        lanes = slice(i * LANES, (i + 1) * LANES)
        total = own_ref[:, lanes]
        for one in got:
            total = total + one[i * share : (i + 1) * share, :].astype(F32)
        scale = packed[i : i + 1, :] * form / samples + epsilon
        out_ref[lanes, :] = (total * lax.rsqrt(scale)).T


def final(samp, own, extra, got, traits, samples):
    share, variants = own.shape
    return pl.pallas_call(
        functools.partial(final_kernel, len(got), traits, samples),
        out_shape=jax.ShapeDtypeStruct((variants, share), F32),
        in_specs=[SMEM] + [VMEM] * (2 + len(got)),
        out_specs=VMEM,
        name="final",
    )(samp, own, extra, *got)


def shift(count, inner, outer_hop, inner_hop):
    outer = count // inner
    pairs = []
    for source in range(count):
        o, i = divmod(source, inner)
        pairs.append(
            (source, (o + outer_hop) % outer * inner + (i + inner_hop) % inner)
        )
    return pairs


def inner_factor(count):
    inner = 1
    while (inner * 2) ** 2 <= count and count % (inner * 2) == 0:
        inner *= 2
    return inner


def solution(mesh):
    n_samp, n_var = mesh.shape["samp"], mesh.shape["var"]
    inner = inner_factor(n_var)
    outer = n_var // inner
    cores = 2 if n_samp % 2 == 0 else 1
    chips = n_samp // cores

    def local(phenotype, inverse_blocks, bin_sizes, slot_of, dosages):
        width, traits = phenotype.shape
        samples = slot_of.shape[0]
        samp, var = lax.axis_index("samp"), lax.axis_index("var")
        own = whiten(bin_sizes, phenotype, inverse_blocks)

        of_bin, of_row = slot_of // width, slot_of % width
        hop_outer = (var // inner - of_bin // inner) % outer
        hop_inner = (var % inner - of_bin % inner) % inner
        place = hop_inner * outer + hop_outer
        slots = (place * width + of_row).reshape(1, samples)
        arranged = arrange(slots, dosages, n_var * width)

        order = sorted(range(1, outer), key=lambda k: min(k, outer - k))
        line = {0: own}
        for k in order:
            line[k] = lax.ppermute(own, "var", shift(n_var, inner, k, 0))
        side = []
        for h in range(1, inner):
            pairs = shift(n_var, inner, 0, h)
            passed = {k: lax.ppermute(line[k], "var", pairs) for k in [0] + order}
            side += [passed[k] for k in range(outer)]
        near = [line[k] for k in range(outer)]
        score, extra = score_first(near, arranged, traits)
        core = (samp % cores).reshape(1)
        chip = (samp // cores).reshape(1)
        send, keep, extra = score_last(
            core, side, outer, arranged, score, extra, chips, cores
        )
        got = [
            lax.ppermute(send[h - 1], "samp", shift(n_samp, cores, 0, h))
            for h in range(1, cores)
        ]
        share = traits // n_samp
        send, mine, extra = middle(chip, keep, extra, got, chips, share)
        got = [
            lax.ppermute(send[h - 1], "samp", shift(n_samp, cores, h, 0))
            for h in range(1, chips)
        ]
        return final(samp.reshape(1), mine, extra, got, traits, samples * n_samp)

    in_specs = (
        P(("samp", "var"), None),
        P(("samp", "var"), None, None),
        P("samp", "var"),
        P("samp"),
        P("samp", "var"),
    )
    return jax.shard_map(
        local, mesh=mesh, in_specs=in_specs, out_specs=P("var", "samp"), check_vma=False
    )
```

time: 118 us -> 58.4 us (0.49)
  blocking collectives: 66.9 us -> 0 us
  Pallas kernels: 0 us -> 26.4 us
  between operations: 14.2 us -> 0.74 us
  local copies, waits for them, and re-layouts: 18 us -> 4.63 us
  starting transfers between devices: 0.04 us -> 12.6 us
  matrix products: 7.78 us -> 0 us
  waiting for transfers between devices: 8.19 us -> 13 us
  other arithmetic: 2.53 us -> 0.73 us
    psum x2 -> x0, blocking collectives: 44.6 us -> none  [the longest x1 38.1 us: local(): lax.psum(jnp.sum(masked_pheno * whitened, axis=0), ('samp', 'var'))]
    pallas_call x0 -> x6, Pallas kernels: none -> 26.4 us  [the longest x1 10.5 us: arrange(): pl.pallas_call(arrange_kernel, out_shape=jax.ShapeDtypeStruct((slot_count...]
    all_gather x1 -> x0, blocking collectives: 22.3 us -> none  [local(): lax.all_gather(slot_weight, 'var', axis=0, tiled=True)]
    gather x3 -> x0, local copies, waits for them, and re-layouts: 17.7 us -> none  [the longest x1 9.46 us: local(): sample_weight = jnp.take(weights_all, slot_of).astype(jnp.float32)]
    ppermute x0 -> x9, waiting for transfers between devices: none -> 13 us  [the longest x3 6.66 us: local(): line[k] = lax.ppermute(own, 'var', shift(n_var, inner, k, 0))]
    ppermute x0 -> x9, starting transfers between devices: none -> 12.6 us  [the longest x3 6.09 us: local(): line[k] = lax.ppermute(own, 'var', shift(n_var, inner, k, 0))]
    all_gather x1 -> x0, waiting for transfers between devices: 8.15 us -> none  [local(): lax.all_gather(white_rows, 'var', axis=0, tiled=True)]
    dot_general x3 -> x0, matrix products: 7.78 us -> none  [the longest x1 3.22 us: local(): lax.dot_general(dosages, picked, (((0,), (0,)), ((), ())), preferred_elem...]
  transfers between devices with their start and end apart: 2 -> 9, of which waited for: 1 -> 4; matrix products, arithmetic and copies ran while one was open for 13% -> 2% of each run, Pallas kernels for 0% -> 26%
where the time goes in v1:
time: 58.4 us; the launch traced here: 58.1 us
  Pallas kernels  26.4 us (45%)
  waiting for transfers between devices  13 us (22%)
  starting transfers between devices  12.6 us (22%)
  local copies, waits for them, and re-layouts  4.63 us (8%)
  between operations  0.74 us (1%)
  other arithmetic  0.73 us (1%)
    pallas_call x1, Pallas kernels, arrange(): pl.pallas_call(arrange_kernel, out_shape=jax.ShapeDtypeStruct((slot_count...  10.5 us
    ppermute x3, waiting for transfers between devices, local(): line[k] = lax.ppermute(own, 'var', shift(n_var, inner, k, 0))  6.66 us
    ppermute x3, starting transfers between devices, local(): line[k] = lax.ppermute(own, 'var', shift(n_var, inner, k, 0))  6.09 us
    pallas_call x1, Pallas kernels, score_last(): pl.pallas_call(functools.partial(score_last_kernel, count, first, chips,...  5.07 us
    ppermute x4, starting transfers between devices, local(): passed = {k: lax.ppermute(line[k], 'var', pairs) for k in [0] + order}  5.06 us
    pallas_call x1, Pallas kernels, score_first(): pl.pallas_call(functools.partial(score_first_kernel, count), out_shape=(j...  4.74 us
    ppermute x1, waiting for transfers between devices, local(): lax.ppermute(send[h - 1], 'samp', shift(n_samp, cores, h, 0))  4.52 us
    unnamed x18, local copies, waits for them, and re-layouts  2.1 us
  transfers between devices with their start and end apart: 9, of which 4 were waited for; matrix products, arithmetic and copies ran while one was open for 2% of the time, Pallas kernels for 26%

profile of v1, /device:TPU:0, one launch (start us, length us, event | category | flops | bytes accessed | tf_op | source)
XLA Modules:
  0.0 58.1 jit_solution(1744025595926270775)
XLA Ops:
  0.7 2.0 %whiten.1.refs_0_ = bf16[272,256]{1,0:T(8,128)(2,1)} custom-call(s32[1,1]{1,0:T(1,128)S(6)} %copy.7.size_ref, bf16[256,256]{1,0:T(8,128)(2,1)} %pheno_ref.1, f32[1,256,256]{2,1,0:T(8,128)} %inverse_ref.1), custom_call_target="tpu_custom_call" | custom-call | tf_op jit(solution)/shard_map/whiten/pallas_call | solution.py:60
  2.7 5.1 %collective-permute-start.5 = (bf16[272,256]{1,0:T(8,128)(2,1)}, bf16[272,256]{1,0:T(8,128)(2,1)S(1)}, u32[]{:S(2)}, u32[]{:S(2)}) collective-permute-start(bf16[272,256]{1,0:T(8,128)(2,1)} %whiten.1.refs_0_), channel_id=1, source_target_pairs={{0,6},{1,7},{2,0},{3,1},{4,2},{5,3},{6,4},{7,5},{8,14},{9,15},{10,... | collective-permute-start | bytes 417800 | tf_op jit(solution)/shard_map/ppermute | solution.py:392
  7.8 1.0 %collective-permute-start.1 = (bf16[272,256]{1,0:T(8,128)(2,1)}, bf16[272,256]{1,0:T(8,128)(2,1)S(1)}, u32[]{:S(2)}, u32[]{:S(2)}) collective-permute-start(bf16[272,256]{1,0:T(8,128)(2,1)} %whiten.1.refs_0_), channel_id=1, source_target_pairs={{0,2},{1,3},{2,4},{3,5},{4,6},{5,7},{6,0},{7,1},{8,10},{9,11},{10,... | collective-permute-start | bytes 417800 | tf_op jit(solution)/shard_map/ppermute | solution.py:392
  8.8 1.5 %collective-permute-start = (bf16[272,256]{1,0:T(8,128)(2,1)}, bf16[272,256]{1,0:T(8,128)(2,1)S(1)}, u32[]{:S(2)}, u32[]{:S(2)}) collective-permute-start(bf16[272,256]{1,0:T(8,128)(2,1)} %whiten.1.refs_0_), channel_id=1, source_target_pairs={{0,1},{1,0},{2,3},{3,2},{4,5},{5,4},{6,7},{7,6},{8,9},{9,8},{10,11... | collective-permute-start | bytes 417800 | tf_op jit(solution)/shard_map/ppermute | solution.py:396
  10.3 0.7 %fusion.5 = s32[1536]{0:T(1024)S(1)} fusion(s32[1536]{0:T(1024)} %param.8, s32[]{:T(128)S(6)} %select_n.50, s32[]{:T(128)S(6)} %select_n.46), kind=kLoop, calls=%fused_computation.21 | loop fusion | flops 101376 | bytes 12296 | tf_op jit(solution)/shard_map/add | solution.py:386
  11.0 0.6 %reshape.15.slot_ref = s32[1,1536]{1,0:T(1,128)} reshape(s32[1536]{0:T(1024)S(1)} %fusion.5) | data formatting | bytes 12288 | tf_op jit(solution)/shard_map/reshape | solution.py:386
  11.6 0.5 collective-permute-done.5.refs_3_
  12.2 1.5 %collective-permute-start.6 = (bf16[272,256]{1,0:T(8,128)(2,1)S(1)}, bf16[272,256]{1,0:T(8,128)(2,1)S(1)}, u32[]{:S(2)}, u32[]{:S(2)}) collective-permute-start(bf16[272,256]{1,0:T(8,128)(2,1)S(1)} %collective-permute-done.5.refs_3_), channel_id=1, source_target_pairs={{0,1},{1,0},{2,3},{3,2},{4,5},{5,4},{6,7},{7,6},{8,9},{9,8},{10,11... | collective-permute-start | bytes 417800 | tf_op jit(solution)/shard_map/ppermute | solution.py:396
  13.7 6.1 %collective-permute-done.3.refs_2_ = bf16[272,256]{1,0:T(8,128)(2,1)S(1)} collective-permute-done((bf16[272,256]{1,0:T(8,128)(2,1)}, bf16[272,256]{1,0:T(8,128)(2,1)S(1)}, u32[]{:S(2)}, u32[]{:S(2)}) %collective-permute-start.3) | collective-permute-done | bytes 139296 | tf_op jit(solution)/shard_map/ppermute | solution.py:392
  19.8 1.5 %collective-permute-start.4 = (bf16[272,256]{1,0:T(8,128)(2,1)S(1)}, bf16[272,256]{1,0:T(8,128)(2,1)S(1)}, u32[]{:S(2)}, u32[]{:S(2)}) collective-permute-start(bf16[272,256]{1,0:T(8,128)(2,1)S(1)} %collective-permute-done.3.refs_2_), channel_id=1, source_target_pairs={{0,1},{1,0},{2,3},{3,2},{4,5},{5,4},{6,7},{7,6},{8,9},{9,8},{10,11... | collective-permute-start | bytes 417800 | tf_op jit(solution)/shard_map/ppermute | solution.py:396
  21.3 0.5 collective-permute-start.2
  21.8 10.5 %arrange.1.refs_4_.refs_5_ = bf16[2048,1024]{1,0:T(8,128)(2,1)} custom-call(s32[1,1536]{1,0:T(1,128)} %reshape.15.slot_ref, bf16[1536,1024]{1,0:T(8,128)(2,1)} %dosage_ref.1), custom_call_target="tpu_custom_call" | custom-call | flops 6442450944 | bytes 7340032 | tf_op jit(solution)/shard_map/arrange/pallas_call | solution.py:92
  32.4 4.7 %score_first.1 = (f32[256,1024]{1,0:T(8,128)}, f32[24,1024]{1,0:T(8,128)}) custom-call(bf16[272,256]{1,0:T(8,128)(2,1)} %whiten.1.refs_0_, bf16[272,256]{1,0:T(8,128)(2,1)} %copy-done.5, bf16[272,256]{1,0:T(8,128)(2,1)} %copy-done.4, bf16[272,256]{1,0:T(8,128)(2,1)} %copy-done.3, bf16[2048,1024]{1,0:T(8,128)(2,1)} %arrange.1.refs_4_.refs_5_), custom_call_target="tpu_custom_call" | custom-call | flops 1073741824 | bytes 4194304 | tf_op jit(solution)/shard_map/score_first/pallas_call | solution.py:152
  37.2 0.6 %copy-done.2 = bf16[272,256]{1,0:T(8,128)(2,1)} copy-done((bf16[272,256]{1,0:T(8,128)(2,1)}, bf16[272,256]{1,0:T(8,128)(2,1)S(1)}, u32[]{:S(2)}) %copy-start.2) | copy-done | bytes 139288
  37.8 0.1 copy-done.8
  37.9 5.1 %score_last.1 = (bf16[1,1072,128]{2,1,0:T(8,128)(2,1)}, f32[128,1024]{1,0:T(8,128)}, f32[16,128]{1,0:T(8,128)}) custom-call(s32[1]{0:T(128)} %bitcast.2.refs_0_, bf16[272,256]{1,0:T(8,128)(2,1)} %copy-done.2, bf16[272,256]{1,0:T(8,128)(2,1)} %copy-done.8, bf16[272,256]{1,0:T(8,128)(2,1)} %copy-done.7, bf16[272,256]{1,0:T(8,128)(2,1)} %copy-done.6, ...), custom_call_target="tpu_custom_call" | custom-call | tf_op jit(solution)/shard_map/score_last/pallas_call | solution.py:249
  43.0 1.8 %collective-permute-done.7.refs_3_ = bf16[1072,128]{1,0:T(8,128)(2,1)S(1)} collective-permute-done((bf16[1072,128]{1,0:T(8,128)(2,1)}, bf16[1072,128]{1,0:T(8,128)(2,1)S(1)}, u32[]{:S(2)}, u32[]{:S(2)}) %collective-permute-start.7) | collective-permute-done | bytes 274464 | tf_op jit(solution)/shard_map/ppermute | solution.py:406
  44.7 0.7 %copy-done = bf16[1072,128]{1,0:T(8,128)(2,1)} copy-done((bf16[1072,128]{1,0:T(8,128)(2,1)}, bf16[1072,128]{1,0:T(8,128)(2,1)S(1)}, u32[]{:S(2)}) %copy-start) | copy-done | bytes 274456
  45.4 1.9 %middle.1 = (bf16[1,560,128]{2,1,0:T(8,128)(2,1)}, f32[64,1024]{1,0:T(8,128)}, f32[16,128]{1,0:T(8,128)}) custom-call(s32[1]{0:T(128)} %bitcast.1.refs_0_, f32[128,1024]{1,0:T(8,128)} %get-tuple-element.15.refs_1_, f32[16,128]{1,0:T(8,128)} %get-tuple-element.16.refs_2_, bf16[1072,128]{1,0:T(8,128)(2,1)} %copy-done), custom_call_target="tpu_custom_call" | custom-call | tf_op jit(solution)/shard_map/middle/pallas_call | solution.py:299
  47.4 1.5 %collective-permute-start.8 = (bf16[560,128]{1,0:T(8,128)(2,1)}, bf16[560,128]{1,0:T(8,128)(2,1)S(1)}, u32[]{:S(2)}, u32[]{:S(2)}) collective-permute-start(bf16[560,128]{1,0:T(8,128)(2,1)} %bitcast.6), channel_id=1, source_target_pairs={{0,16},{8,24},{16,0},{24,8},{1,17},{9,25},{17,1},{25,9},{2,18},{10... | collective-permute-start | bytes 430088 | tf_op jit(solution)/shard_map/ppermute | solution.py:412
  48.9 4.5 %collective-permute-done.8.refs_3_ = bf16[560,128]{1,0:T(8,128)(2,1)S(1)} collective-permute-done((bf16[560,128]{1,0:T(8,128)(2,1)}, bf16[560,128]{1,0:T(8,128)(2,1)S(1)}, u32[]{:S(2)}, u32[]{:S(2)}) %collective-permute-start.8) | collective-permute-done | bytes 143392 | tf_op jit(solution)/shard_map/ppermute | solution.py:412
  53.4 0.6 %copy-done.1 = bf16[560,128]{1,0:T(8,128)(2,1)} copy-done((bf16[560,128]{1,0:T(8,128)(2,1)}, bf16[560,128]{1,0:T(8,128)(2,1)S(1)}, u32[]{:S(2)}) %copy-start.1) | copy-done | bytes 143384
  54.0 2.1 %final.1 = f32[1024,64]{1,0:T(8,128)} custom-call(s32[1]{0:T(128)} %bitcast.refs_0_, f32[64,1024]{1,0:T(8,128)} %get-tuple-element.18.refs_1_, f32[16,128]{1,0:T(8,128)} %get-tuple-element.19.refs_2_, bf16[560,128]{1,0:T(8,128)(2,1)} %copy-done.1), custom_call_target="tpu_custom_call" | custom-call | tf_op jit(solution)/shard_map/final/pallas_call | solution.py:342
  56.1 1.9 %copy.6 = f32[1024,64]{0,1:T(8,128)} copy(f32[1024,64]{1,0:T(8,128)} %final.1) | data formatting | bytes 524288 | tf_op jit(solution)/shard_map/final/pallas_call | solution.py:342
  (21 shorter events, 0.1 us)
Async XLA Ops:
  2.7 9.5 %collective-permute-start.5 = (bf16[272,256]{1,0:T(8,128)(2,1)}, bf16[272,256]{1,0:T(8,128)(2,1)S(1)}, u32[]{:S(2)}, u32[]{:S(2)}) collective-permute-start(bf16[272,256]{1,0:T(8,128)(2,1)} %whiten.1.refs_0_), channel_id=1, source_target_pairs={{0,6},{1,7},{2,0},{3,1},{4,2},{5,3},{6,4},{7,5},{8,14},{9,15},{10,... | collective-permute-start | bytes 417800 | tf_op jit(solution)/shard_map/ppermute | solution.py:392
  7.8 12.0 %collective-permute-start.3 = (bf16[272,256]{1,0:T(8,128)(2,1)}, bf16[272,256]{1,0:T(8,128)(2,1)S(1)}, u32[]{:S(2)}, u32[]{:S(2)}) collective-permute-start(bf16[272,256]{1,0:T(8,128)(2,1)} %whiten.1.refs_0_), channel_id=1, source_target_pairs={{0,4},{1,5},{2,6},{3,7},{4,0},{5,1},{6,2},{7,3},{8,12},{9,13},{10,... | collective-permute-start | bytes 417800 | tf_op jit(solution)/shard_map/ppermute | solution.py:392
  7.8 13.6 %collective-permute-start.1 = (bf16[272,256]{1,0:T(8,128)(2,1)}, bf16[272,256]{1,0:T(8,128)(2,1)S(1)}, u32[]{:S(2)}, u32[]{:S(2)}) collective-permute-start(bf16[272,256]{1,0:T(8,128)(2,1)} %whiten.1.refs_0_), channel_id=1, source_target_pairs={{0,2},{1,3},{2,4},{3,5},{4,6},{5,7},{6,0},{7,1},{8,10},{9,11},{10,... | collective-permute-start | bytes 417800 | tf_op jit(solution)/shard_map/ppermute | solution.py:392
  8.8 28.3 %collective-permute-start = (bf16[272,256]{1,0:T(8,128)(2,1)}, bf16[272,256]{1,0:T(8,128)(2,1)S(1)}, u32[]{:S(2)}, u32[]{:S(2)}) collective-permute-start(bf16[272,256]{1,0:T(8,128)(2,1)} %whiten.1.refs_0_), channel_id=1, source_target_pairs={{0,1},{1,0},{2,3},{3,2},{4,5},{5,4},{6,7},{7,6},{8,9},{9,8},{10,11... | collective-permute-start | bytes 417800 | tf_op jit(solution)/shard_map/ppermute | solution.py:396
  12.2 20.2 %copy-start.3 = (bf16[272,256]{1,0:T(8,128)(2,1)}, bf16[272,256]{1,0:T(8,128)(2,1)S(1)}, u32[]{:S(2)}) copy-start(bf16[272,256]{1,0:T(8,128)(2,1)S(1)} %collective-permute-done.5.refs_3_) | copy-start | bytes 417796
  12.2 24.9 %collective-permute-start.6 = (bf16[272,256]{1,0:T(8,128)(2,1)S(1)}, bf16[272,256]{1,0:T(8,128)(2,1)S(1)}, u32[]{:S(2)}, u32[]{:S(2)}) collective-permute-start(bf16[272,256]{1,0:T(8,128)(2,1)S(1)} %collective-permute-done.5.refs_3_), channel_id=1, source_target_pairs={{0,1},{1,0},{2,3},{3,2},{4,5},{5,4},{6,7},{7,6},{8,9},{9,8},{10,11... | collective-permute-start | bytes 417800 | tf_op jit(solution)/shard_map/ppermute | solution.py:396
  19.8 12.5 %copy-start.4 = (bf16[272,256]{1,0:T(8,128)(2,1)}, bf16[272,256]{1,0:T(8,128)(2,1)S(1)}, u32[]{:S(2)}) copy-start(bf16[272,256]{1,0:T(8,128)(2,1)S(1)} %collective-permute-done.3.refs_2_) | copy-start | bytes 417796
  19.8 17.3 %collective-permute-start.4 = (bf16[272,256]{1,0:T(8,128)(2,1)S(1)}, bf16[272,256]{1,0:T(8,128)(2,1)S(1)}, u32[]{:S(2)}, u32[]{:S(2)}) collective-permute-start(bf16[272,256]{1,0:T(8,128)(2,1)S(1)} %collective-permute-done.3.refs_2_), channel_id=1, source_target_pairs={{0,1},{1,0},{2,3},{3,2},{4,5},{5,4},{6,7},{7,6},{8,9},{9,8},{10,11... | collective-permute-start | bytes 417800 | tf_op jit(solution)/shard_map/ppermute | solution.py:396
  21.3 11.0 %copy-start.5 = (bf16[272,256]{1,0:T(8,128)(2,1)}, bf16[272,256]{1,0:T(8,128)(2,1)S(1)}, u32[]{:S(2)}) copy-start(bf16[272,256]{1,0:T(8,128)(2,1)S(1)} %collective-permute-done.1.refs_1_) | copy-start | bytes 417796
  21.3 15.8 %collective-permute-start.2 = (bf16[272,256]{1,0:T(8,128)(2,1)S(1)}, bf16[272,256]{1,0:T(8,128)(2,1)S(1)}, u32[]{:S(2)}, u32[]{:S(2)}) collective-permute-start(bf16[272,256]{1,0:T(8,128)(2,1)S(1)} %collective-permute-done.1.refs_1_), channel_id=1, source_target_pairs={{0,1},{1,0},{2,3},{3,2},{4,5},{5,4},{6,7},{7,6},{8,9},{9,8},{10,11... | collective-permute-start | bytes 417800 | tf_op jit(solution)/shard_map/ppermute | solution.py:396
  37.1 0.7 %copy-start.2 = (bf16[272,256]{1,0:T(8,128)(2,1)}, bf16[272,256]{1,0:T(8,128)(2,1)S(1)}, u32[]{:S(2)}) copy-start(bf16[272,256]{1,0:T(8,128)(2,1)S(1)} %collective-permute-done.refs_1_) | copy-start | bytes 417796
  37.1 0.7 %copy-start.6 = (bf16[272,256]{1,0:T(8,128)(2,1)}, bf16[272,256]{1,0:T(8,128)(2,1)S(1)}, u32[]{:S(2)}) copy-start(bf16[272,256]{1,0:T(8,128)(2,1)S(1)} %collective-permute-done.6.refs_4_) | copy-start | bytes 417796
  37.1 0.7 %copy-start.7 = (bf16[272,256]{1,0:T(8,128)(2,1)}, bf16[272,256]{1,0:T(8,128)(2,1)S(1)}, u32[]{:S(2)}) copy-start(bf16[272,256]{1,0:T(8,128)(2,1)S(1)} %collective-permute-done.4.refs_3_) | copy-start | bytes 417796
  37.1 0.7 %copy-start.8 = (bf16[272,256]{1,0:T(8,128)(2,1)}, bf16[272,256]{1,0:T(8,128)(2,1)S(1)}, u32[]{:S(2)}) copy-start(bf16[272,256]{1,0:T(8,128)(2,1)S(1)} %collective-permute-done.2.refs_2_) | copy-start | bytes 417796
  43.0 1.8 %collective-permute-start.7 = (bf16[1072,128]{1,0:T(8,128)(2,1)}, bf16[1072,128]{1,0:T(8,128)(2,1)S(1)}, u32[]{:S(2)}, u32[]{:S(2)}) collective-permute-start(bf16[1072,128]{1,0:T(8,128)(2,1)} %bitcast.5), channel_id=1, source_target_pairs={{0,8},{8,0},{16,24},{24,16},{1,9},{9,1},{17,25},{25,17},{2,10},{10... | collective-permute-start | bytes 823304 | tf_op jit(solution)/shard_map/ppermute | solution.py:406
  44.7 0.7 %copy-start = (bf16[1072,128]{1,0:T(8,128)(2,1)}, bf16[1072,128]{1,0:T(8,128)(2,1)S(1)}, u32[]{:S(2)}) copy-start(bf16[1072,128]{1,0:T(8,128)(2,1)S(1)} %collective-permute-done.7.refs_3_) | copy-start | bytes 823300
  47.4 6.0 %collective-permute-start.8 = (bf16[560,128]{1,0:T(8,128)(2,1)}, bf16[560,128]{1,0:T(8,128)(2,1)S(1)}, u32[]{:S(2)}, u32[]{:S(2)}) collective-permute-start(bf16[560,128]{1,0:T(8,128)(2,1)} %bitcast.6), channel_id=1, source_target_pairs={{0,16},{8,24},{16,0},{24,8},{1,17},{9,25},{17,1},{25,9},{2,18},{10... | collective-permute-start | bytes 430088 | tf_op jit(solution)/shard_map/ppermute | solution.py:412
  53.4 0.7 %copy-start.1 = (bf16[560,128]{1,0:T(8,128)(2,1)}, bf16[560,128]{1,0:T(8,128)(2,1)S(1)}, u32[]{:S(2)}) copy-start(bf16[560,128]{1,0:T(8,128)(2,1)S(1)} %collective-permute-done.8.refs_3_) | copy-start | bytes 430084
